TPU v7x, 32 devices: a whole 2x2x4 slice. The times are simulated.
32 devices in a mesh: island: 4 (over y, core), shard: 8 (over z, x).
Axes of the slice: x: 2, y: 2, z: 4, core: 2. Of those that a mesh axis runs over, the one named last changes fastest.
Arguments:
- pseudo_grad: float32 [4, 2048, 4096], P('island', 'shard'), may hold values from -6 to 6
- error_buffer: float32 [4, 2048, 4096], P('island', 'shard'), may hold values from -6 to 6
- momentum: float32 [2048, 4096], P('shard'), may hold values from -4 to 4
- weights: bfloat16 [2048, 4096], P('shard'), may hold values from -6 to 6
- warm_basis: float32 [2048, 64], P('shard'), may hold values from -6 to 6
Outputs:
- new_error: float32 [4, 2048, 4096], P('island', 'shard')
- new_momentum: float32 [2048, 4096], P('shard')
- new_weights: bfloat16 [2048, 4096], P('shard')
- new_basis: float32 [2048, 64], P('shard')
All inputs are finite; a program needn't handle non-finite values.
Results may differ from a plain program's by a relative error of at most 0.001.
Values sent between devices are 32-bit elements; how exact they have to be, the bound alone decides.
A program may use at most 128 MiB of HBM per device.

v0:
```python
import jax
import jax.numpy as jnp
from jax import lax
from jax.sharding import PartitionSpec as P

ITERS = 2
HIGH = lax.Precision.HIGHEST
outer_beta = 0.9
outer_rate = 0.7


def orthonormal(factor_rows):
    gram_matrix = jnp.dot(factor_rows, factor_rows.T, precision=HIGH)
    lower_factor = jnp.linalg.cholesky(gram_matrix)
    return lax.linalg.triangular_solve(lower_factor, factor_rows, left_side=True, lower=True)


def on_device(pseudo_grad, error_buffer, momentum, weights, warm_basis):
    merged = (pseudo_grad + error_buffer)[0]
    basis_now = warm_basis
    for iteration in range(ITERS):
        partial_value = lax.dot_general(basis_now, merged, (((0,), (0,)), ((), ())), precision=HIGH)
        factor_rows = orthonormal(lax.psum(partial_value, ("island", "shard")))
        local_proj = lax.dot_general(merged, factor_rows, (((1,), (1,)), ((), ())), precision=HIGH)
        basis_now = lax.psum(local_proj, "island")
    new_error = merged - jnp.dot(local_proj, factor_rows, precision=HIGH)
    update = jnp.dot(basis_now / lax.axis_size("island"), factor_rows, precision=HIGH)
    new_momentum = outer_beta * momentum + update
    stepped = weights.astype(jnp.float32) - outer_rate * (update + outer_beta * new_momentum)
    return (new_error[None], new_momentum, stepped.astype(jnp.bfloat16), basis_now)


def solution(mesh):
    in_specs = (
        P("island", "shard", None),
        P("island", "shard", None),
        P("shard", None),
        P("shard", None),
        P("shard", None),
    )
    out_specs = (P("island", "shard", None), P("shard", None), P("shard", None), P("shard", None))
    return jax.shard_map(
        on_device, mesh=mesh, in_specs=in_specs, out_specs=out_specs, check_vma=False
    )
```

profile of v0, /device:TPU:0, one launch (start us, length us, event | category | flops | bytes accessed | tf_op | source)
XLA Modules:
  0.0 420.1 jit_solution(8857783116008560494)
XLA Ops:
  7.2 0.0 all-reduce.5.cloned.1.call-start
  7.2 3.9 add.25
  11.2 2.0 copy-done.1
  13.2 3.8 convolution_bitcast_fusion
  17.0 0.0 all-reduce.5.cloned.1.call-update
  17.0 0.0 all-reduce.7.cloned.1.call-start
  17.1 133.6 %all-reduce.5.cloned.1.call-done = f32[64,4096]{1,0:T(8,128)} async-done(((f32[64,4096]{1,0:T(8,128)}), f32[64,4096]{1,0:T(8,128)}) %all-reduce.5.cloned.1.call-update) | async-done | bytes 1048592 | tf_op jit(solution)/shard_map/psum | solution.py:23
  150.7 2.5 fusion.22
  153.3 0.1 copy.9
  153.3 5.8 %cholesky.44 = f32[64,64]{1,0:T(8,128)S(1)} custom-call(f32[64,64]{1,0:T(8,128)S(1)} %fusion.17), custom_call_target="Cholesky" | custom-call | tf_op jit(solution)/shard_map/jit(cholesky)/cholesky | solution.py:14
  159.2 0.6 compare_reduce_fusion.1
  159.9 0.7 fusion.10
  160.5 4.9 %custom-call.6 = f32[1,64,64]{1,2,0:T(8,128)S(1)} custom-call(f32[1,64,64]{2,1,0:T(8,128)S(1)} %fusion.10), custom_call_target="InvertDiagBlocksLowerTriangular" | custom-call | tf_op jit(solution)/shard_map/triangular_solve/custom-call.0 | solution.py:15
  165.4 2.3 fusion.15
  167.7 5.8 %fusion.5 = f32[256,64]{1,0:T(8,128)} fusion(f32[64,4096]{1,0:T(8,128)S(1)} %fusion.15, f32[1,256,4096]{2,1,0:T(8,128)} %copy-done.1), kind=kOutput, calls=%fused_computation.7 | convolution fusion | flops 805306368 | bytes 5308416 | tf_op jit(solution)/shard_map/dot_general | solution.py:24
  173.6 0.2 all-reduce.9.cloned.1.call-start
  173.8 30.7 %all-reduce.7.cloned.1.call-done = f32[256,64]{1,0:T(8,128)} async-done(((f32[256,64]{1,0:T(8,128)}), f32[256,64]{1,0:T(8,128)}) %all-reduce.7.cloned.1.call-update) | async-done | bytes 65552 | tf_op jit(solution)/shard_map/psum | solution.py:25
  204.4 5.9 %fusion.3 = f32[64,4096]{1,0:T(8,128)} fusion(f32[256,64]{1,0:T(8,128)} %all-reduce.7.cloned.1.call-done, f32[1,256,4096]{2,1,0:T(8,128)} %copy-done.1), kind=kOutput, calls=%fused_computation.5 | convolution fusion | flops 805306368 | bytes 5308416 | tf_op jit(solution)/shard_map/dot_general | solution.py:22
  210.3 130.9 %all-reduce.9.cloned.1.call-done = f32[64,4096]{1,0:T(8,128)} async-done(((f32[64,4096]{1,0:T(8,128)}), f32[64,4096]{1,0:T(8,128)}) %all-reduce.9.cloned.1.call-update) | async-done | bytes 1048592 | tf_op jit(solution)/shard_map/psum | solution.py:23
  341.2 2.5 fusion.23
  343.8 0.1 copy.10
  343.9 5.8 %cholesky.55 = f32[64,64]{1,0:T(8,128)S(1)} custom-call(f32[64,64]{1,0:T(8,128)S(1)} %fusion.14), custom_call_target="Cholesky" | custom-call | tf_op jit(solution)/shard_map/jit(cholesky)/cholesky | solution.py:14
  349.7 0.6 compare_reduce_fusion
  350.4 0.7 fusion.11
  351.1 4.9 %custom-call.7 = f32[1,64,64]{1,2,0:T(8,128)S(1)} custom-call(f32[1,64,64]{2,1,0:T(8,128)S(1)} %fusion.11), custom_call_target="InvertDiagBlocksLowerTriangular" | custom-call | tf_op jit(solution)/shard_map/triangular_solve/custom-call.0 | solution.py:15
  355.9 2.3 fusion.12
  358.2 6.1 %fusion.1 = f32[256,64]{0,1:T(8,128)S(1)} fusion(f32[64,4096]{1,0:T(8,128)S(1)} %fusion.12, f32[1,256,4096]{2,1,0:T(8,128)} %copy-done.1), kind=kOutput, calls=%fused_computation.3 | convolution fusion | flops 805306368 | bytes 5308416 | tf_op jit(solution)/shard_map/dot_general | solution.py:24
  364.4 6.8 %fusion = f32[1,256,4096]{2,1,0:T(8,128)} fusion(f32[256,64]{0,1:T(8,128)S(1)} %fusion.1, f32[64,4096]{1,0:T(8,128)S(1)} %fusion.12, f32[1,256,4096]{2,1,0:T(8,128)} %copy-done.1), kind=kOutput, calls=%fused_computation.1 | convolution fusion | flops 806354944 | bytes 9502720 | tf_op jit(solution)/shard_map/dot_general | solution.py:26
  371.1 0.6 all-reduce.11.cloned.1.call-update
  371.7 33.3 %all-reduce.11.cloned.1.call-done = f32[256,64]{0,1:T(8,128)} async-done(((f32[256,64]{0,1:T(8,128)}), f32[256,64]{0,1:T(8,128)}) %all-reduce.11.cloned.1.call-update) | async-done | bytes 65552 | tf_op jit(solution)/shard_map/psum | solution.py:25
  405.0 7.9 %subtract_convert_fusion = (bf16[256,4096]{1,0:T(8,128)(2,1)}, f32[256,4096]{1,0:T(8,128)}) fusion(bf16[256,4096]{1,0:T(8,128)(2,1)S(1)} %copy-done.2, f32[256,4096]{1,0:T(8,128)} %param.10, f32[64,4096]{1,0:T(8,128)S(1)} %fusion.12, f32[256,64]{0,1:T(8,128)} %all-reduce.11.cloned.1.call-done), kind=kOutput, calls=%fused_computation.10 | convolution fusion | flops 813711360 | bytes 13697024 | tf_op jit(solution)/shard_map/dot_general | solution.py:27
  412.9 0.6 copy.15
  (16 shorter events, 0.1 us)
Async XLA Ops:
  7.2 6.0 %copy-start = (f32[256,64]{0,1:T(8,128)S(1)}, f32[256,64]{0,1:T(8,128)}, u32[]{:S(2)}) copy-start(f32[256,64]{0,1:T(8,128)} %param.12) | copy-start | bytes 196612
  7.2 143.5 %all-reduce.5.cloned.1.call-start = ((), (), s32[]{:S(2)}) async-start(), calls=%async_computation | async-start | bytes 2097152 | tf_op jit(solution)/shard_map/psum | solution.py:23
  11.2 2.0 copy-start.1
  17.0 187.4 %all-reduce.7.cloned.1.call-start = ((), (), s32[]{:S(2)}) async-start(), calls=%async_computation.1 | async-start | bytes 262144 | tf_op jit(solution)/shard_map/psum | solution.py:25
  173.6 167.7 %all-reduce.9.cloned.1.call-start = ((), (), s32[]{:S(2)}) async-start(), calls=%async_computation.2 | async-start | bytes 2097152 | tf_op jit(solution)/shard_map/psum | solution.py:23
  364.3 6.8 %copy-start.3 = (f32[256,64]{0,1:T(8,128)}, f32[256,64]{0,1:T(8,128)S(1)}, u32[]{:S(2)}) copy-start(f32[256,64]{0,1:T(8,128)S(1)} %fusion.1) | copy-start | bytes 196612
  364.3 40.7 %copy-start.2 = (bf16[256,4096]{1,0:T(8,128)(2,1)S(1)}, bf16[256,4096]{1,0:T(8,128)(2,1)}, u32[]{:S(2)}) copy-start(bf16[256,4096]{1,0:T(8,128)(2,1)} %param.11) | copy-start | bytes 6291460
  371.1 33.9 %all-reduce.11.cloned.1.call-start = ((), (), s32[]{:S(2)}) async-start(), calls=%async_computation.3 | async-start | bytes 131072 | tf_op jit(solution)/shard_map/psum | solution.py:25
  405.0 7.9 %copy-start.4 = (f32[256,64]{0,1:T(8,128)S(1)}, f32[256,64]{0,1:T(8,128)}, u32[]{:S(2)}) copy-start(f32[256,64]{0,1:T(8,128)} %all-reduce.11.cloned.1.call-done) | copy-start | bytes 196612
Sparse Core Ops, SparseCore 0:
  17.2 133.5 all-reduce.4
  173.7 30.7 all-reduce.6
  210.5 130.7 all-reduce.8
  374.5 30.4 all-reduce.10
where the time goes:
time: 420 us
  waiting for transfers between devices  329 us (78%)
  matrix products  45.8 us (11%)
  other arithmetic  28.1 us (7%)
  between operations  13.9 us (3%)
    psum x2, waiting for transfers between devices, on_device(): factor_rows = orthonormal(lax.psum(partial_value, ('island', 'shard')))  265 us
    psum x2, waiting for transfers between devices, on_device(): basis_now = lax.psum(local_proj, 'island')  64 us
    another operation x6, other arithmetic, orthonormal(): lower_factor = jnp.linalg.cholesky(gram_matrix)  13 us
    dot_general x2, matrix products, on_device(): lax.dot_general(merged, factor_rows, (((1,), (1,)), ((), ())), precision=...  11.9 us
    another operation x4, other arithmetic, orthonormal(): lax.linalg.triangular_solve(lower_factor, factor_rows, left_side=True, lo...  11.1 us
    dot_general x2, matrix products, on_device(): lax.dot_general(basis_now, merged, (((0,), (0,)), ((), ())), precision=HIGH)  9.69 us
  transfers between devices with their start and end apart: 4, of which 4 were waited for; matrix products, arithmetic and copies ran while one was open for 0% of the time, Pallas kernels for 0%

commit v1 on v0

--- a/solution.py
+++ b/solution.py
@@ -22,7 +22,11 @@
         partial_value = lax.dot_general(basis_now, merged, (((0,), (0,)), ((), ())), precision=HIGH)
         factor_rows = orthonormal(lax.psum(partial_value, ("island", "shard")))
         local_proj = lax.dot_general(merged, factor_rows, (((1,), (1,)), ((), ())), precision=HIGH)
-        basis_now = lax.psum(local_proj, "island")
+        basis_now = local_proj
+        for hop in (1, 2):
+            basis_now = basis_now + lax.ppermute(
+                basis_now, "island", [(dev, dev ^ hop) for dev in range(4)]
+            )
     new_error = merged - jnp.dot(local_proj, factor_rows, precision=HIGH)
     update = jnp.dot(basis_now / lax.axis_size("island"), factor_rows, precision=HIGH)
     new_momentum = outer_beta * momentum + update

time: 420 us -> 358 us (0.85)
  waiting for transfers between devices: 329 us -> 268 us
  matrix products: 45.8 us -> 41.2 us
    psum x2 -> x0, waiting for transfers between devices: 64 us -> none  [on_device(): basis_now = lax.psum(local_proj, 'island')]
    ppermute x0 -> x4, waiting for transfers between devices: none -> 5.32 us  [on_device(): lax.ppermute(basis_now, 'island', [(dev, dev ^ hop) for dev in range(4)])]
  transfers between devices with their start and end apart: 4 -> 6, of which waited for: 4 -> 5; matrix products, arithmetic and copies ran while one was open for 0% -> 1% of each run, Pallas kernels for 0% -> 0%
where the time goes in v1:
time: 358 us
  waiting for transfers between devices  268 us (75%)
  matrix products  41.2 us (12%)
  other arithmetic  28.1 us (8%)
  between operations  14.2 us (4%)
    psum x2, waiting for transfers between devices, on_device(): factor_rows = orthonormal(lax.psum(partial_value, ('island', 'shard')))  263 us
    another operation x6, other arithmetic, orthonormal(): lower_factor = jnp.linalg.cholesky(gram_matrix)  13 us
    dot_general x2, matrix products, on_device(): lax.dot_general(merged, factor_rows, (((1,), (1,)), ((), ())), precision=...  12.2 us
    another operation x4, other arithmetic, orthonormal(): lax.linalg.triangular_solve(lower_factor, factor_rows, left_side=True, lo...  11.1 us
    dot_general x2, matrix products, on_device(): lax.dot_general(basis_now, merged, (((0,), (0,)), ((), ())), precision=HIGH)  7.43 us
  transfers between devices with their start and end apart: 6, of which 5 were waited for; matrix products, arithmetic and copies ran while one was open for 1% of the time, Pallas kernels for 0%

profile of v1, /device:TPU:0, one launch (start us, length us, event | category | flops | bytes accessed | tf_op | source)
XLA Modules:
  0.0 357.6 jit_solution(14821967077679782719)
XLA Ops:
  7.2 3.9 %add.33 = f32[1,256,4096]{2,1,0:T(8,128)S(1)} add(f32[1,256,4096]{2,1,0:T(8,128)} %param.8, f32[1,256,4096]{2,1,0:T(8,128)} %param.9) | non-fusion elementwise | flops 1048576 | bytes 12582912 | tf_op jit(solution)/shard_map/add | solution.py:19
  11.2 2.0 copy-done.1
  13.2 3.8 %convolution_bitcast_fusion = f32[64,4096]{1,0:T(8,128)} fusion(f32[256,64]{0,1:T(8,128)S(1)} %copy-done, f32[1,256,4096]{2,1,0:T(8,128)S(1)} %add.33), kind=kOutput, calls=%fused_computation.2 | convolution fusion | flops 805306368 | bytes 5308416 | tf_op jit(solution)/shard_map/dot_general | solution.py:22
  17.0 0.2 all-reduce.5.cloned.1.call-start
  17.3 133.3 %all-reduce.3.cloned.1.call-done = f32[64,4096]{1,0:T(8,128)} async-done(((f32[64,4096]{1,0:T(8,128)}), f32[64,4096]{1,0:T(8,128)}) %all-reduce.3.cloned.1.call-update) | async-done | bytes 1048592 | tf_op jit(solution)/shard_map/psum | solution.py:23
  150.6 2.5 fusion.23
  153.1 0.1 copy.9
  153.2 5.8 %cholesky.44 = f32[64,64]{1,0:T(8,128)S(1)} custom-call(f32[64,64]{1,0:T(8,128)S(1)} %fusion.18), custom_call_target="Cholesky" | custom-call | tf_op jit(solution)/shard_map/jit(cholesky)/cholesky | solution.py:14
  159.1 0.6 compare_reduce_fusion.1
  159.7 0.7 fusion.11
  160.4 4.9 %custom-call.6 = f32[1,64,64]{1,2,0:T(8,128)S(1)} custom-call(f32[1,64,64]{2,1,0:T(8,128)S(1)} %fusion.11), custom_call_target="InvertDiagBlocksLowerTriangular" | custom-call | tf_op jit(solution)/shard_map/triangular_solve/custom-call.0 | solution.py:15
  165.3 2.4 fusion.16
  167.7 6.1 %fusion.5 = f32[256,64]{0,1:T(8,128)S(1)} fusion(f32[64,4096]{1,0:T(8,128)S(1)} %fusion.16, f32[1,256,4096]{2,1,0:T(8,128)} %copy-done.1), kind=kOutput, calls=%fused_computation.7 | convolution fusion | flops 805306368 | bytes 5308416 | tf_op jit(solution)/shard_map/dot_general | solution.py:24
  173.9 0.1 collective-permute-start
  173.9 1.2 collective-permute-done
  175.2 1.5 collective-permute-start.1
  176.7 2.8 collective-permute-done.1
  179.5 3.6 %fusion.3 = f32[64,4096]{1,0:T(8,128)} fusion(f32[1,256,4096]{2,1,0:T(8,128)S(1)} %copy-done.2, f32[256,64]{0,1:T(8,128)S(1)} %add.34, f32[256,64]{0,1:T(8,128)S(1)} %collective-permute-done.1), kind=kOutput, calls=%fused_computation.5 | convolution fusion | flops 805322752 | bytes 5373952 | tf_op jit(solution)/shard_map/dot_general | solution.py:22
  183.1 129.8 %all-reduce.5.cloned.1.call-done = f32[64,4096]{1,0:T(8,128)} async-done(((f32[64,4096]{1,0:T(8,128)}), f32[64,4096]{1,0:T(8,128)}) %all-reduce.5.cloned.1.call-update) | async-done | bytes 1048592 | tf_op jit(solution)/shard_map/psum | solution.py:23
  312.9 2.5 fusion.24
  315.5 0.1 copy.10
  315.5 5.8 %cholesky.55 = f32[64,64]{1,0:T(8,128)S(1)} custom-call(f32[64,64]{1,0:T(8,128)S(1)} %fusion.15), custom_call_target="Cholesky" | custom-call | tf_op jit(solution)/shard_map/jit(cholesky)/cholesky | solution.py:14
  321.4 0.6 compare_reduce_fusion
  322.1 0.7 fusion.12
  322.7 4.9 %custom-call.7 = f32[1,64,64]{1,2,0:T(8,128)S(1)} custom-call(f32[1,64,64]{2,1,0:T(8,128)S(1)} %fusion.12), custom_call_target="InvertDiagBlocksLowerTriangular" | custom-call | tf_op jit(solution)/shard_map/triangular_solve/custom-call.0 | solution.py:15
  327.6 2.6 fusion.13
  330.3 6.1 %fusion.1 = f32[256,64]{0,1:T(8,128)S(1)} fusion(f32[64,4096]{1,0:T(8,128)S(1)} %fusion.13, f32[1,256,4096]{2,1,0:T(8,128)} %copy-done.1), kind=kOutput, calls=%fused_computation.3 | convolution fusion | flops 805306368 | bytes 5308416 | tf_op jit(solution)/shard_map/dot_general | solution.py:24
  336.4 0.1 collective-permute-start.2
  336.5 1.2 collective-permute-done.2
  337.8 1.5 collective-permute-start.3
  339.3 5.1 %fusion = f32[1,256,4096]{2,1,0:T(8,128)} fusion(f32[256,64]{0,1:T(8,128)S(1)} %fusion.1, f32[64,4096]{1,0:T(8,128)S(1)} %fusion.13, f32[1,256,4096]{2,1,0:T(8,128)S(1)} %copy-done.3), kind=kOutput, calls=%fused_computation.1 | convolution fusion | flops 806354944 | bytes 9502720 | tf_op jit(solution)/shard_map/dot_general | solution.py:30
  344.4 6.4 %subtract_convert_fusion = (bf16[256,4096]{1,0:T(8,128)(2,1)}, f32[256,4096]{1,0:T(8,128)}) fusion(bf16[256,4096]{1,0:T(8,128)(2,1)S(1)} %copy-done.5, f32[256,4096]{1,0:T(8,128)S(1)} %copy-done.4, f32[64,4096]{1,0:T(8,128)S(1)} %fusion.13, f32[256,64]{0,1:T(8,128)S(1)} %add.37), kind=kOutput, calls=%fused_computation.10 | convolution fusion | flops 813711360 | bytes 13697024 | tf_op jit(solution)/shard_map/dot_general | solution.py:31
  (24 shorter events, 0.2 us)
Async XLA Ops:
  7.2 6.0 %copy-start = (f32[256,64]{0,1:T(8,128)S(1)}, f32[256,64]{0,1:T(8,128)}, u32[]{:S(2)}) copy-start(f32[256,64]{0,1:T(8,128)} %param.12) | copy-start | bytes 196612
  7.2 143.4 %all-reduce.3.cloned.1.call-start = ((), (), s32[]{:S(2)}) async-start(), calls=%async_computation | async-start | bytes 2097152 | tf_op jit(solution)/shard_map/psum | solution.py:23
  11.2 2.0 copy-start.1
  17.0 295.9 %all-reduce.5.cloned.1.call-start = ((), (), s32[]{:S(2)}) async-start(), calls=%async_computation.1 | async-start | bytes 2097152 | tf_op jit(solution)/shard_map/psum | solution.py:23
  165.3 14.2 %copy-start.2 = (f32[1,256,4096]{2,1,0:T(8,128)S(1)}, f32[1,256,4096]{2,1,0:T(8,128)}, u32[]{:S(2)}) copy-start(f32[1,256,4096]{2,1,0:T(8,128)} %copy-done.1) | copy-start | bytes 12582916
  173.9 1.3 collective-permute-start
  175.2 4.3 %collective-permute-start.1 = (f32[256,64]{0,1:T(8,128)S(1)}, f32[256,64]{0,1:T(8,128)S(1)}, u32[]{:S(2)}, u32[]{:S(2)}) collective-permute-start(f32[256,64]{0,1:T(8,128)S(1)} %add.34), channel_id=1, source_target_pairs={{0,16},{8,24},{16,0},{24,8},{1,17},{9,25},{17,1},{25,9},{2,18},{10... | collective-permute-start | bytes 196616 | tf_op jit(solution)/shard_map/ppermute | solution.py:27
  327.6 11.6 %copy-start.3 = (f32[1,256,4096]{2,1,0:T(8,128)S(1)}, f32[1,256,4096]{2,1,0:T(8,128)}, u32[]{:S(2)}) copy-start(f32[1,256,4096]{2,1,0:T(8,128)} %copy-done.1) | copy-start | bytes 12582916
  336.4 1.3 collective-permute-start.2
  337.7 6.7 %copy-start.4 = (f32[256,4096]{1,0:T(8,128)S(1)}, f32[256,4096]{1,0:T(8,128)}, u32[]{:S(2)}) copy-start(f32[256,4096]{1,0:T(8,128)} %param.10) | copy-start | bytes 12582916
  337.8 6.7 %copy-start.5 = (bf16[256,4096]{1,0:T(8,128)(2,1)S(1)}, bf16[256,4096]{1,0:T(8,128)(2,1)}, u32[]{:S(2)}) copy-start(bf16[256,4096]{1,0:T(8,128)(2,1)} %param.11) | copy-start | bytes 6291460
  337.8 6.6 %collective-permute-start.3 = (f32[256,64]{0,1:T(8,128)S(1)}, f32[256,64]{0,1:T(8,128)S(1)}, u32[]{:S(2)}, u32[]{:S(2)}) collective-permute-start(f32[256,64]{0,1:T(8,128)S(1)} %add.36), channel_id=1, source_target_pairs={{0,16},{8,24},{16,0},{24,8},{1,17},{9,25},{17,1},{25,9},{2,18},{10... | collective-permute-start | bytes 196616 | tf_op jit(solution)/shard_map/ppermute | solution.py:27
  344.4 6.4 %copy-start.6 = (f32[256,64]{0,1:T(8,128)}, f32[256,64]{0,1:T(8,128)S(1)}, u32[]{:S(2)}) copy-start(f32[256,64]{0,1:T(8,128)S(1)} %add.37) | copy-start | bytes 196612
Sparse Core Ops, SparseCore 0:
  17.2 133.3 all-reduce.2
  183.3 129.6 all-reduce.4
